TPU v7x, 128 devices: a 2x2x16 block of a 8x8x16 slice. The times are simulated.
128 devices in a mesh: groups: 4 (over x, y), wide: 32 (over z, core).
Axes of the slice: x: 2, y: 2, z: 16, core: 2. Of those that a mesh axis runs over, the one named last changes fastest.
The devices are a block of a 8x8x16 slice.
Arguments:
- half_integrals: float32 [1024, 512, 800], P(('groups', 'wide')), parts along dimension 0, may hold values from -40 to 40
- pair_list: int32 [1024, 2], P('groups'), parts along dimension 0, may hold values from 0 to 199, as said below
- occupied_energy: float32 [800], P('groups'), parts along dimension 0, may hold values from -3 to -0.3
- virtual_orbitals: float32 [3200, 600], P('groups'), parts along dimension 0, may hold values from -0.21875 to 0.21875
- tile_order: int32 [64], replicated, may hold values from 0 to 63, each once
Outputs:
- transformed: float32 [1024, 512, 600], P('groups', 'wide'), parts along dimension 0
- pair_rms: float32 [1024], P('groups'), parts along dimension 0
There are 4 independent parts, one for each index of `groups`. A program takes and returns all parts, laid end to end along the dimension named above; an argument that names none is the same for every part. Nothing has to cross between parts.
Inputs may be any that keep to these rules, and one draw needn't show every extreme that they name: `pair_list`: each row is a distinct pair (i, j) with i <= j.
All inputs are finite; a program needn't handle non-finite values.
Results may differ from a plain program's by a relative error of at most 0.00007.
Values sent between devices are 32-bit elements; how exact they have to be, the bound alone decides.
No kernel may reach another device: no remote copies, remote signals or barrier semaphores. Data moves between devices by JAX's collectives and lax.ppermute only.
A program may use at most 128 MiB of HBM per device.

v0:
```python
import functools

import jax
import jax.numpy as jnp
from jax import lax
from jax.experimental import pallas as pl
from jax.experimental.pallas import tpu as pltpu
from jax.sharding import PartitionSpec as P


TILE_S = 8
LANES = 128
CHUNKS = 5
AHEAD = 2
STEP = 40
PACK = 280
UNPACK = 80
LAST = 40
UNROLL = 2
EARLY = (1, 2, 4)


SMEM = pl.BlockSpec(memory_space=pltpu.SMEM)
VMEM = pl.BlockSpec(memory_space=pltpu.VMEM)
ANY = pl.BlockSpec(memory_space=pl.ANY)


def pair_weights(pair_list, occupied_energy):
    orbital = jnp.arange(occupied_energy.shape[0], dtype=jnp.int32)
    first = jnp.sum(
        jnp.where(pair_list[:, 0:1] == orbital[None, :], occupied_energy[None, :], 0.0), axis=1
    )
    second = jnp.sum(
        jnp.where(pair_list[:, 1:2] == orbital[None, :], occupied_energy[None, :], 0.0), axis=1
    )
    return jnp.exp(0.3 * (first + second))


def split(x):
    high = x.astype(jnp.bfloat16)
    return high, (x - high.astype(jnp.float32)).astype(jnp.bfloat16)


def product_of(v_high, v_low, high, low):
    dot = functools.partial(jnp.dot, preferred_element_type=jnp.float32)
    return dot(v_high, low) + dot(v_low, high) + dot(v_high, high)


def turned(rows, turn):
    lane = lax.broadcasted_iota(jnp.int32, (rows, LANES), 1)
    return (lane - turn + LANES) % LANES


def paired_order(lane, pairs):
    half = pairs * TILE_S
    return (lane // half) * half + (lane % pairs) * TILE_S + (lane // pairs) % TILE_S


def own_turn(pos, pairs):
    return lax.rem(pos[0] * pairs, LANES)


def take_lanes(x, index):
    return jnp.take_along_axis(x, index, axis=1, mode="promise_in_bounds")


def early_kernel(shifts, peers, first, pos, order, half, *refs):
    n = len(shifts)
    if first:
        orbitals, refs = refs[0], refs[1:]
        outs, kept = refs[:n], refs[n : n + 2]
        data, high, low, sems, v_in, v_high, v_low, v_sems = refs[n + 2 :]
    else:
        v_high, v_low = refs[:2]
        outs = refs[2 : n + 2]
        data, high, low, sems = refs[n + 2 :]
    pairs, basis, _ = data.shape
    rows_out = outs[0].shape[0]
    span = basis // CHUNKS

    def piece(c):
        rows = pl.ds(pl.multiple_of(c * span, span), span)
        return pltpu.make_async_copy(half.at[:, rows, :], data.at[:, rows, :], sems.at[c])

    if first:
        v_copy = pltpu.make_async_copy(orbitals, v_in, v_sems.at[0])
        v_copy.start()
    for c in range(AHEAD):
        piece(c).start()
    if first:
        v_copy.wait()
        v_high[...], v_low[...] = split(v_in[...].T)
        keep = [
            pltpu.make_async_copy(x, y, v_sems.at[1 + m])
            for m, (x, y) in enumerate(zip((v_high, v_low), kept))
        ]
    group = lax.broadcasted_iota(jnp.int32, (span, LANES), 1) // TILE_S
    index = paired_order(turned(span, own_turn(pos, pairs)), pairs)
    per_block = LANES // TILE_S
    sources = []
    for shift in shifts:
        owner = lax.rem(pos[0] + shift, peers)
        for h in range(2):
            tile = order[2 * owner + h]
            start = pl.multiple_of((tile // per_block) * LANES, LANES)
            sources.append((start, h * pairs, lax.rem(tile, per_block)))

    def gather(step, carry):
        piece(step).wait()

        @pl.when(step + AHEAD < CHUNKS)
        def _():
            piece(step + AHEAD).start()

        rows = pl.ds(pl.multiple_of(step * span, span), span)
        for n in range(len(shifts)):
            block = None
            for start, base, place in sources[2 * n : 2 * n + 2]:
                for p in range(pairs):
                    amount = lax.rem((base + p - place + per_block) * TILE_S, LANES)
                    x = pltpu.roll(data[p, rows, pl.ds(start, LANES)], amount, 1)
                    block = x if block is None else jnp.where(group == base + p, x, block)
            columns = pl.ds(n * LANES, LANES)
            high[rows, columns], low[rows, columns] = split(take_lanes(block, index))
        return carry

    lax.fori_loop(0, CHUNKS, gather, 0)
    if first:
        for copy in keep:
            copy.start()
    product = product_of(v_high[:rows_out], v_low[:rows_out], high[...], low[...])
    for m in range(n):
        outs[m][...] = product[:, m * LANES : (m + 1) * LANES]
    if first:
        for copy in keep:
            copy.wait()


def early_blocks(shifts, peers, cut, pos, order, half, *orbitals):
    pairs, basis, columns = half.shape
    first = len(orbitals) == 1
    virtuals = orbitals[0].shape[1 if first else 0]
    n = len(shifts)
    more = [jax.ShapeDtypeStruct((virtuals, basis), jnp.bfloat16)] * 2 if first else []
    return pl.pallas_call(
        functools.partial(early_kernel, shifts, peers, first),
        in_specs=[SMEM, SMEM, ANY] + [ANY if first else VMEM] * len(orbitals),
        out_specs=[VMEM] * n + [ANY] * len(more),
        out_shape=[jax.ShapeDtypeStruct((cut, LANES), jnp.float32)] * n + more,
        scratch_shapes=[
            pltpu.VMEM((pairs, basis, columns), jnp.float32),
            pltpu.VMEM((basis, n * LANES), jnp.bfloat16),
            pltpu.VMEM((basis, n * LANES), jnp.bfloat16),
            pltpu.SemaphoreType.DMA((CHUNKS,)),
        ]
        + (
            [
                pltpu.VMEM((basis, virtuals), jnp.float32),
                pltpu.VMEM((virtuals, basis), jnp.bfloat16),
                pltpu.VMEM((virtuals, basis), jnp.bfloat16),
                pltpu.SemaphoreType.DMA((3,)),
            ]
            if first
            else []
        ),
        cost_estimate=pl.CostEstimate(
            flops=6 * n * LANES * basis * virtuals,
            bytes_accessed=4 * pairs * basis * columns,
            transcendentals=0,
        ),
    )(pos, order, half, *orbitals)


def rest_kernel(shifts, peers, skipped, pos, order, half, v_high, v_low, *refs):
    n = len(shifts) - skipped
    outs = refs[:n]
    ends, squares, products, tiles = refs[n:]
    pairs, virtuals, columns = products.shape
    steps = (virtuals - LAST) // PACK
    step = pl.program_id(0)
    blocks = columns // LANES
    per_block = LANES // TILE_S

    @pl.when(step < pairs)
    def _():
        high, low = split(half[0])
        product = product_of(v_high[...], v_low[...], high, low)
        products[step] = product
        sums = jnp.sum((product * product).reshape(virtuals // 8, 8, columns), axis=0)
        total = sums[:, :LANES]
        for b in range(1, blocks):
            total = total + sums[:, b * LANES : (b + 1) * LANES]
        squares[0] = total

    group = lax.broadcasted_iota(jnp.int32, (STEP, LANES), 1) // TILE_S
    turn = own_turn(pos, pairs)
    index = paired_order(turned(STEP, 0), pairs)
    front = turned(STEP, turn) < LANES // 2

    def source(owner, h):
        tile = order[2 * owner + h]
        within = lax.rem(tile, per_block)
        place = (tile // per_block) * pairs + lax.rem(within, pairs)
        return place, lax.rem(lax.rem(within // pairs + h, 2) * (LANES // 2) + turn, LANES)

    def block_for(owner):
        a, turn_a = source(owner, 0)
        c, turn_c = source(owner, 1)
        return jnp.where(front, pltpu.roll(tiles[a], turn_a, 1), pltpu.roll(tiles[c], turn_c, 1))

    def fill(row):
        rows_in = pl.ds(pl.multiple_of(row, 8), STEP)

        def one(b, carry):
            columns_in = pl.ds(pl.multiple_of(b * LANES, LANES), LANES)
            x = [products[p, rows_in, columns_in] for p in range(pairs)]
            m = 1
            while m < pairs:
                upper = (group & m) != 0
                y = list(x)
                for p in range(pairs):
                    if not p & m:
                        q = p | m
                        y[p] = jnp.where(upper, pltpu.roll(x[q], TILE_S * m, 1), x[p])
                        y[q] = jnp.where(upper, x[q], pltpu.roll(x[p], LANES - TILE_S * m, 1))
                x = y
                m *= 2
            for p in range(pairs):
                tiles[b * pairs + p] = take_lanes(x[p], index)
            return carry

        lax.fori_loop(0, blocks, one, 0)

    @pl.when((step >= pairs) & (step < pairs + steps))
    def _():
        def one(i, carry):
            fill((step - pairs) * PACK + i * STEP)
            rows_out = pl.ds(pl.multiple_of(i * STEP, 8), STEP)
            for j, shift in enumerate(shifts[skipped:]):
                outs[j][rows_out, :] = block_for(lax.rem(pos[0] + shift, peers))
            return carry

        lax.fori_loop(0, PACK // STEP, one, 0)

    @pl.when(step == pairs + steps)
    def _():
        fill(virtuals - LAST)

        def one(owner, carry):
            ends[owner] = block_for(owner)
            return carry

        lax.fori_loop(0, peers, one, 0)


def rest_blocks(shifts, peers, skipped, pos, order, half, v_high, v_low):
    pairs, basis, columns = half.shape
    virtuals = v_high.shape[0]
    n = len(shifts) - skipped
    cut = virtuals - LAST
    steps = cut // PACK
    results = pl.pallas_call(
        functools.partial(rest_kernel, shifts, peers, skipped),
        grid=(pairs + steps + 1,),
        in_specs=[
            SMEM,
            SMEM,
            pl.BlockSpec((1, basis, columns), lambda i: (jnp.minimum(i, pairs - 1), 0, 0)),
        ]
        + [pl.BlockSpec((virtuals, basis), lambda i: (0, 0))] * 2,
        out_specs=[pl.BlockSpec((PACK, LANES), lambda i: (jnp.clip(i - pairs, 0, steps - 1), 0))] * n
        + [
            pl.BlockSpec((peers, LAST, LANES), lambda i: (0, 0, 0)),
            pl.BlockSpec((1, 8, LANES), lambda i: (jnp.minimum(i, pairs - 1), 0, 0)),
        ],
        out_shape=[jax.ShapeDtypeStruct((cut, LANES), jnp.float32)] * n
        + [
            jax.ShapeDtypeStruct((peers, LAST, LANES), jnp.float32),
            jax.ShapeDtypeStruct((pairs, 8, LANES), jnp.float32),
        ],
        scratch_shapes=[
            pltpu.VMEM((pairs, virtuals, columns), jnp.float32),
            pltpu.VMEM((columns * pairs // LANES, STEP, LANES), jnp.float32),
        ],
        cost_estimate=pl.CostEstimate(
            flops=6 * pairs * columns * basis * virtuals,
            bytes_accessed=4 * pairs * basis * columns,
            transcendentals=0,
        ),
        name="rest_blocks",
    )(pos, order, half, v_high, v_low)
    return results[:n], results[n], results[n + 1]


def merge(x, pairs, ahead):
    n = len(x)
    group = lax.broadcasted_iota(jnp.int32, x[0].shape, 1) // pairs
    behind = (group - ahead + n) % n
    m = 1
    while m < n:
        far = (behind & m) != 0
        x = [jnp.where(far, x[(j + m) % n], x[j]) for j in range(n)]
        m *= 2
    turns = [(LANES - k * pairs) % LANES for k in range(n)]
    return [pltpu.roll(x[-k % n], t, 1) if t else x[0] for k, t in enumerate(turns)]


def unpack_kernel(peers, pairs, pos, weights, *refs):
    ins, out = refs[:peers], refs[-1]
    per = LANES // pairs
    ahead = lax.rem(pos[0], per)
    outer = lax.div(pos[0], per)
    group = lax.broadcasted_iota(jnp.int32, (8, LANES), 1) // pairs
    straight = group >= ahead
    count = peers // per

    def one(step, carry):
        for t in range(UNROLL):
            rows = pl.ds(pl.multiple_of((step * UNROLL + t) * 8, 8), 8)
            halves = [
                merge([ins[b * per + j][rows, :] for j in range(per)], pairs, ahead)
                for b in range(count)
            ]
            for b in range(count):
                place = pl.multiple_of(lax.rem(b + outer, count) * LANES, LANES)
                scale = weights[:, pl.ds(place, LANES)]
                for k in range(per):
                    value = jnp.where(straight, halves[b][k], halves[b - 1][k])
                    out[k, rows, pl.ds(place, LANES)] = value * scale
        return carry

    lax.fori_loop(0, out.shape[1] // (8 * UNROLL), one, 0)


def unpack(blocks, pos, weights, pairs, virtuals):
    peers = len(blocks)
    per = LANES // pairs
    total = weights.shape[1]
    return pl.pallas_call(
        functools.partial(unpack_kernel, peers, pairs),
        grid=(blocks[0].shape[0] // UNPACK,),
        in_specs=[SMEM, pl.BlockSpec((1, total), lambda i: (0, 0))]
        + [pl.BlockSpec((UNPACK, LANES), lambda i: (i, 0))] * peers,
        out_specs=pl.BlockSpec((per, UNPACK, total), lambda i: (0, i, 0)),
        out_shape=jax.ShapeDtypeStruct((per, virtuals, total), jnp.float32),
        name="unpack",
    )(pos, weights, *blocks)


def unpack_last_kernel(pairs, weights, ends, _, out):
    peers, rows, _ = ends.shape
    per = LANES // pairs

    def one(step, carry):
        at = pl.ds(pl.multiple_of(step * 8, 8), 8)
        for b in range(peers // per):
            lanes = pl.ds(b * LANES, LANES)
            done = merge([ends[b * per + j, at, :] for j in range(per)], pairs, 0)
            for k in range(per):
                out[k, at, lanes] = done[k] * weights[:, lanes]
        return carry

    lax.fori_loop(0, rows // 8, one, 0, unroll=True)


def unpack_last(ends, weights, pairs, into):
    per, virtuals, total = into.shape
    rows = ends.shape[1]
    return pl.pallas_call(
        functools.partial(unpack_last_kernel, pairs),
        grid=(1,),
        in_specs=[
            pl.BlockSpec((1, total), lambda i: (0, 0)),
            pl.BlockSpec(ends.shape, lambda i: (0, 0, 0)),
            ANY,
        ],
        out_specs=pl.BlockSpec((per, rows, total), lambda i: (0, virtuals // rows - 1, 0)),
        out_shape=jax.ShapeDtypeStruct(into.shape, into.dtype),
        input_output_aliases={2: 0},
        name="unpack_last",
    )(weights, ends, into)


def order_of_shifts(peers):
    shifts = [peers // 2]
    for d in range(peers // 2 - 1, 0, -1):
        shifts += [d, peers - d]
    return shifts + [0]


def shards(half_integrals, pair_list, occupied_energy, virtual_orbitals, tile_order):
    pairs, columns, _ = half_integrals.shape
    virtuals = virtual_orbitals.shape[1]
    peers = lax.axis_size("wide")
    cut = virtuals - LAST
    pos = lax.axis_index("wide").astype(jnp.int32).reshape(1)
    half = jnp.swapaxes(half_integrals, 1, 2)
    shifts = tuple(order_of_shifts(peers))
    blocks = []
    kept = [virtual_orbitals]
    at = 0
    for n in EARLY:
        results = early_blocks(shifts[at : at + n], peers, cut, pos, tile_order, half, *kept)
        blocks += results[:n]
        kept = results[n:] or kept
        at += n
    more, ends, sums = rest_blocks(shifts, peers, at, pos, tile_order, half, *kept)
    blocks += more
    arrived = {}
    for n, s in enumerate(shifts):
        block = blocks[n]
        if s:
            block = lax.ppermute(block, "wide", [(i, (i + s) % peers) for i in range(peers)])
        arrived[(peers - s) % peers] = block
    squares = jnp.sum(sums, axis=(1, 2))
    sent = jnp.broadcast_to(squares[None, None], (peers, 1, pairs))
    totals = lax.all_to_all(sent, "wide", 0, 0, tiled=True).reshape(peers * pairs)
    ends = lax.all_to_all(ends, "wide", 0, 0, tiled=True)
    weights = pair_weights(pair_list, occupied_energy)
    pair_rms = jnp.sqrt(totals * weights * weights / (columns * virtuals) + 1e-06)
    out = unpack([arrived[i] for i in range(peers)], pos, weights[None], pairs, virtuals)
    out = unpack_last(ends, weights[None], pairs, out)
    return (jnp.transpose(out, (2, 0, 1)), pair_rms)


def solution(mesh):
    in_specs = (
        P(("groups", "wide"), None, None),
        P("groups", None),
        P("groups"),
        P("groups", None),
        P(),
    )
    out_specs = (P("groups", "wide", None), P("groups"))
    return jax.shard_map(shards, mesh=mesh, in_specs=in_specs, out_specs=out_specs, check_vma=False)
```

profile of v0, /device:TPU:196, one launch (start us, length us, event | category | flops | bytes accessed | tf_op | source)
XLA Modules:
  0.0 658.6 jit_solution(7544525051486781543)
XLA Ops:
  0.6 9.7 %shard_map.68 = (f32[560,128]{1,0:T(8,128)}, bf16[600,800]{1,0:T(8,128)(2,1)}, bf16[600,800]{1,0:T(8,128)(2,1)}) custom-call(s32[1]{0:T(128)} %bitcast.3.pos, s32[64]{0:T(128)} %order.7, f32[8,800,512]{2,1,0:T(8,128)} %bitcast.6, f32[800,600]{1,0:T(8,128)} %refs_0_.1), custom_call_target="tpu_custom_call" | custom-call | flops 368640000 | bytes 13107200 | tf_op jit(solution)/shard_map/pallas_call | solution.py:145
  10.4 58.7 %rest_blocks.1 = (f32[560,128]{1,0:T(8,128)}, f32[560,128]{1,0:T(8,128)}, f32[560,128]{1,0:T(8,128)}, f32[560,128]{1,0:T(8,128)}, f32[560,128]{1,0:T(8,128)}, /*...) custom-call(s32[1]{0:T(128)} %bitcast.3.pos, ...), custom_call_target="tpu_custom_call" | custom-call | flops 11796480000 | bytes 13107200 | tf_op jit(solution)/shard_map/rest_blocks/pallas_call | solution.py:262
  70.0 27.8 %all_to_all.10 = f32[32,1,8]{2,1,0:T(1,128)S(1)} all-to-all(f32[32,1,8]{2,1,0:T(1,128)S(1)} %broadcast_in_dim.30), channel_id=1, replica_groups=mesh['groups'=4,'wide'=32] {'wide'}, dimensions={0} | all-to-all | bytes 2048 | tf_op jit(solution)/shard_map/all_to_all | solution.py:417
  103.2 9.7 %collective-permute-start.15 = (f32[560,128]{1,0:T(8,128)S(1)}, f32[560,128]{1,0:T(8,128)S(1)}, u32[]{:S(2)}, u32[]{:S(2)}) collective-permute-start(f32[560,128]{1,0:T(8,128)S(1)} %copy-done.13), channel_id=1, source_target_pairs={{0,16},{1,17},{2,18},{3,19},{4,20},{5,21},{6,22},{7,23},{8,24},{9,... | collective-permute-start | bytes 860168 | tf_op jit(solution)/shard_map/ppermute | solution.py:413
  112.9 10.0 %shard_map.70 = (f32[560,128]{1,0:T(8,128)}, f32[560,128]{1,0:T(8,128)}) custom-call(s32[1]{0:T(128)} %bitcast.3.pos, s32[64]{0:T(128)} %order.7, f32[8,800,512]{2,1,0:T(8,128)} %bitcast.8, bf16[600,800]{1,0:T(8,128)(2,1)} %get-tuple-element.38.v_high.refs_0_, bf16[600,800]{1,0:T(8,128)(2,1)} %get-tuple-element.39.v_low.refs_1_), custom_call_target="tpu_custom_call" | custom-call | flops 737280000 | bytes 13107200 | tf_op jit(solution)/shard_map/pallas_call | solution.py:145
  123.6 8.9 %collective-permute-start.16 = (f32[560,128]{1,0:T(8,128)}, f32[560,128]{1,0:T(8,128)S(1)}, u32[]{:S(2)}, u32[]{:S(2)}) collective-permute-start(f32[560,128]{1,0:T(8,128)} %get-tuple-element.58), channel_id=1, source_target_pairs={{0,15},{1,16},{2,17},{3,18},{4,19},{5,20},{6,21},{7,22},{8,23},{9,... | collective-permute-start | bytes 860168 | tf_op jit(solution)/shard_map/ppermute | solution.py:413
  132.6 14.8 %shard_map.69 = (f32[560,128]{1,0:T(8,128)}, f32[560,128]{1,0:T(8,128)}, f32[560,128]{1,0:T(8,128)}, f32[560,128]{1,0:T(8,128)}) custom-call(s32[1]{0:T(128)} %bitcast.3.pos, s32[64]{0:T(128)} %order.7, f32[8,800,512]{2,1,0:T(8,128)} %bitcast.9, bf16[600,800]{1,0:T(8,128)(2,1)} %get-tuple-element.38.v_high.refs_0_, ...), custom_call_target="tpu_custom_call" | custom-call | flops 1474560000 | bytes 13107200 | tf_op jit(solution)/shard_map/pallas_call | solution.py:145
  149.1 7.8 %collective-permute-start.13 = (f32[560,128]{1,0:T(8,128)}, f32[560,128]{1,0:T(8,128)S(1)}, u32[]{:S(2)}, u32[]{:S(2)}) collective-permute-start(f32[560,128]{1,0:T(8,128)} %get-tuple-element.55), channel_id=1, source_target_pairs={{0,18},{1,19},{2,20},{3,21},{4,22},{5,23},{6,24},{7,25},{8,26},{9,... | collective-permute-start | bytes 860168 | tf_op jit(solution)/shard_map/ppermute | solution.py:413
  156.9 9.5 %collective-permute-done.15.refs_16_ = f32[560,128]{1,0:T(8,128)S(1)} collective-permute-done((f32[560,128]{1,0:T(8,128)S(1)}, f32[560,128]{1,0:T(8,128)S(1)}, u32[]{:S(2)}, u32[]{:S(2)}) %collective-permute-start.15) | collective-permute-done | bytes 286752 | tf_op jit(solution)/shard_map/ppermute | solution.py:413
  166.4 65.9 %collective-permute-done.14.refs_15_ = f32[560,128]{1,0:T(8,128)S(1)} collective-permute-done((f32[560,128]{1,0:T(8,128)}, f32[560,128]{1,0:T(8,128)S(1)}, u32[]{:S(2)}, u32[]{:S(2)}) %collective-permute-start.14) | collective-permute-done | bytes 286752 | tf_op jit(solution)/shard_map/ppermute | solution.py:413
  232.3 9.5 %collective-permute-start = (f32[560,128]{1,0:T(8,128)}, f32[560,128]{1,0:T(8,128)S(1)}, u32[]{:S(2)}, u32[]{:S(2)}) collective-permute-start(f32[560,128]{1,0:T(8,128)} %get-tuple-element.42), channel_id=1, source_target_pairs={{0,31},{1,0},{2,1},{3,2},{4,3},{5,4},{6,5},{7,6},{8,7},{9,8},{10,9... | collective-permute-start | bytes 860168 | tf_op jit(solution)/shard_map/ppermute | solution.py:413
  241.8 14.9 %collective-permute-done.12.refs_13_ = f32[560,128]{1,0:T(8,128)S(1)} collective-permute-done((f32[560,128]{1,0:T(8,128)}, f32[560,128]{1,0:T(8,128)S(1)}, u32[]{:S(2)}, u32[]{:S(2)}) %collective-permute-start.12) | collective-permute-done | bytes 286752 | tf_op jit(solution)/shard_map/ppermute | solution.py:413
  263.5 11.3 %collective-permute-done.13.refs_14_ = f32[560,128]{1,0:T(8,128)S(1)} collective-permute-done((f32[560,128]{1,0:T(8,128)}, f32[560,128]{1,0:T(8,128)S(1)}, u32[]{:S(2)}, u32[]{:S(2)}) %collective-permute-start.13) | collective-permute-done | bytes 286752 | tf_op jit(solution)/shard_map/ppermute | solution.py:413
  274.8 18.2 %collective-permute-start.2 = (f32[560,128]{1,0:T(8,128)}, f32[560,128]{1,0:T(8,128)S(1)}, u32[]{:S(2)}, u32[]{:S(2)}) collective-permute-start(f32[560,128]{1,0:T(8,128)} %get-tuple-element.44), channel_id=1, source_target_pairs={{0,29},{1,30},{2,31},{3,0},{4,1},{5,2},{6,3},{7,4},{8,5},{9,6},{10... | collective-permute-start | bytes 860168 | tf_op jit(solution)/shard_map/ppermute | solution.py:413
  297.3 8.1 %collective-permute-start.6 = (f32[560,128]{1,0:T(8,128)}, f32[560,128]{1,0:T(8,128)}, u32[]{:S(2)}, u32[]{:S(2)}) collective-permute-start(f32[560,128]{1,0:T(8,128)} %get-tuple-element.48), channel_id=1, source_target_pairs={{0,25},{1,26},{2,27},{3,28},{4,29},{5,30},{6,31},{7,0},{8,1},{9,2}... | collective-permute-start | bytes 860168 | tf_op jit(solution)/shard_map/ppermute | solution.py:413
  311.2 12.5 %collective-permute-done.3.refs_4_ = f32[560,128]{1,0:T(8,128)} collective-permute-done((f32[560,128]{1,0:T(8,128)}, f32[560,128]{1,0:T(8,128)}, u32[]{:S(2)}, u32[]{:S(2)}) %collective-permute-start.3) | collective-permute-done | bytes 286752 | tf_op jit(solution)/shard_map/ppermute | solution.py:413
  329.4 6.8 %collective-permute-start.9 = (f32[560,128]{1,0:T(8,128)}, f32[560,128]{1,0:T(8,128)}, u32[]{:S(2)}, u32[]{:S(2)}) collective-permute-start(f32[560,128]{1,0:T(8,128)} %get-tuple-element.51), channel_id=1, source_target_pairs={{0,22},{1,23},{2,24},{3,25},{4,26},{5,27},{6,28},{7,29},{8,30},{9,... | collective-permute-start | bytes 860168 | tf_op jit(solution)/shard_map/ppermute | solution.py:413
  336.3 27.7 %collective-permute-done.5.refs_6_ = f32[560,128]{1,0:T(8,128)} collective-permute-done((f32[560,128]{1,0:T(8,128)}, f32[560,128]{1,0:T(8,128)}, u32[]{:S(2)}, u32[]{:S(2)}) %collective-permute-start.5) | collective-permute-done | bytes 286752 | tf_op jit(solution)/shard_map/ppermute | solution.py:413
  370.7 9.6 %collective-permute-start.11 = (f32[560,128]{1,0:T(8,128)}, f32[560,128]{1,0:T(8,128)}, u32[]{:S(2)}, u32[]{:S(2)}) collective-permute-start(f32[560,128]{1,0:T(8,128)} %get-tuple-element.53), channel_id=1, source_target_pairs={{0,20},{1,21},{2,22},{3,23},{4,24},{5,25},{6,26},{7,27},{8,28},{9,... | collective-permute-start | bytes 860168 | tf_op jit(solution)/shard_map/ppermute | solution.py:413
  380.3 31.7 %collective-permute-done.7.refs_8_ = f32[560,128]{1,0:T(8,128)} collective-permute-done((f32[560,128]{1,0:T(8,128)}, f32[560,128]{1,0:T(8,128)}, u32[]{:S(2)}, u32[]{:S(2)}) %collective-permute-start.7) | collective-permute-done | bytes 286752 | tf_op jit(solution)/shard_map/ppermute | solution.py:413
  412.3 9.6 %collective-permute-done.8.refs_9_ = f32[560,128]{1,0:T(8,128)} collective-permute-done((f32[560,128]{1,0:T(8,128)}, f32[560,128]{1,0:T(8,128)}, u32[]{:S(2)}, u32[]{:S(2)}) %collective-permute-start.8) | collective-permute-done | bytes 286752 | tf_op jit(solution)/shard_map/ppermute | solution.py:413
  422.0 15.0 %collective-permute-start.20 = (f32[560,128]{1,0:T(8,128)}, f32[560,128]{1,0:T(8,128)}, u32[]{:S(2)}, u32[]{:S(2)}) collective-permute-start(f32[560,128]{1,0:T(8,128)} %get-tuple-element.62), channel_id=1, source_target_pairs={{0,11},{1,12},{2,13},{3,14},{4,15},{5,16},{6,17},{7,18},{8,19},{9,... | collective-permute-start | bytes 860168 | tf_op jit(solution)/shard_map/ppermute | solution.py:413
  436.9 27.2 %collective-permute-done.9.refs_10_ = f32[560,128]{1,0:T(8,128)} collective-permute-done((f32[560,128]{1,0:T(8,128)}, f32[560,128]{1,0:T(8,128)}, u32[]{:S(2)}, u32[]{:S(2)}) %collective-permute-start.9) | collective-permute-done | bytes 286752 | tf_op jit(solution)/shard_map/ppermute | solution.py:413
  467.7 7.9 %collective-permute-done.10.refs_11_ = f32[560,128]{1,0:T(8,128)} collective-permute-done((f32[560,128]{1,0:T(8,128)}, f32[560,128]{1,0:T(8,128)}, u32[]{:S(2)}, u32[]{:S(2)}) %collective-permute-start.10) | collective-permute-done | bytes 286752 | tf_op jit(solution)/shard_map/ppermute | solution.py:413
  475.7 7.4 %collective-permute-start.22 = (f32[560,128]{1,0:T(8,128)}, f32[560,128]{1,0:T(8,128)}, u32[]{:S(2)}, u32[]{:S(2)}) collective-permute-start(f32[560,128]{1,0:T(8,128)} %get-tuple-element.64), channel_id=1, source_target_pairs={{0,9},{1,10},{2,11},{3,12},{4,13},{5,14},{6,15},{7,16},{8,17},{9,1... | collective-permute-start | bytes 860168 | tf_op jit(solution)/shard_map/ppermute | solution.py:413
  483.1 49.2 %collective-permute-done.11.refs_12_ = f32[560,128]{1,0:T(8,128)} collective-permute-done((f32[560,128]{1,0:T(8,128)}, f32[560,128]{1,0:T(8,128)}, u32[]{:S(2)}, u32[]{:S(2)}) %collective-permute-start.11) | collective-permute-done | bytes 286752 | tf_op jit(solution)/shard_map/ppermute | solution.py:413
  541.7 16.2 %collective-permute-start.27 = (f32[560,128]{1,0:T(8,128)}, f32[560,128]{1,0:T(8,128)}, u32[]{:S(2)}, u32[]{:S(2)}) collective-permute-start(f32[560,128]{1,0:T(8,128)} %get-tuple-element.69), channel_id=1, source_target_pairs={{0,4},{1,5},{2,6},{3,7},{4,8},{5,9},{6,10},{7,11},{8,12},{9,13},{1... | collective-permute-start | bytes 860168 | tf_op jit(solution)/shard_map/ppermute | solution.py:413
  559.5 36.8 %collective-permute-done.24.refs_25_ = f32[560,128]{1,0:T(8,128)} collective-permute-done((f32[560,128]{1,0:T(8,128)}, f32[560,128]{1,0:T(8,128)}, u32[]{:S(2)}, u32[]{:S(2)}) %collective-permute-start.24) | collective-permute-done | bytes 286752 | tf_op jit(solution)/shard_map/ppermute | solution.py:413
  596.4 10.9 %collective-permute-done.25.refs_26_ = f32[560,128]{1,0:T(8,128)} collective-permute-done((f32[560,128]{1,0:T(8,128)}, f32[560,128]{1,0:T(8,128)}, u32[]{:S(2)}, u32[]{:S(2)}) %collective-permute-start.25) | collective-permute-done | bytes 286752 | tf_op jit(solution)/shard_map/ppermute | solution.py:413
  616.5 13.7 %collective-permute-done.27.refs_28_ = f32[560,128]{1,0:T(8,128)} collective-permute-done((f32[560,128]{1,0:T(8,128)}, f32[560,128]{1,0:T(8,128)}, u32[]{:S(2)}, u32[]{:S(2)}) %collective-permute-start.27) | collective-permute-done | bytes 286752 | tf_op jit(solution)/shard_map/ppermute | solution.py:413
  635.7 7.1 %collective-permute-done.29.refs_30_ = f32[560,128]{1,0:T(8,128)} collective-permute-done((f32[560,128]{1,0:T(8,128)}, f32[560,128]{1,0:T(8,128)}, u32[]{:S(2)}, u32[]{:S(2)}) %collective-permute-start.29) | collective-permute-done | bytes 286752 | tf_op jit(solution)/shard_map/ppermute | solution.py:413
  644.6 10.9 %unpack.1._ = f32[16,600,256]{2,1,0:T(8,128)} custom-call(s32[1]{0:T(128)} %bitcast.3.pos, f32[1,256]{1,0:T(1,128)} %bitcast.11, f32[560,128]{1,0:T(8,128)} %get-tuple-element.41.refs_0_, f32[560,128]{1,0:T(8,128)} %copy-done.8, f32[560,128]{1,0:T(8,128)} %copy-done.9, f32[560,128]{1,0:T(8,128)} %copy-done.10, f32[560,128]{1,0:T(8,128)} %collective-permute-done.3.refs_4_, ...), custom_call_target="tpu_custom_call" | custom-call | tf_op jit(solution)/shard_map/unpack/pallas_call | solution.py:339
  (75 shorter events, 72.3 us)
Async XLA Ops:
  97.9 557.7 %all-to-all-start = ((f32[32,40,128]{2,1,0:T(8,128)}), f32[32,40,128]{2,1,0:T(8,128)S(1)}, u32[]{:S(2)}, u32[]{:S(2)}) async-start(f32[32,40,128]{2,1,0:T(8,128)} %get-tuple-element.40), calls=%async_computation | async-start | bytes 1310720 | tf_op jit(solution)/shard_map/all_to_all | solution.py:418
  103.2 63.3 %collective-permute-start.15 = (f32[560,128]{1,0:T(8,128)S(1)}, f32[560,128]{1,0:T(8,128)S(1)}, u32[]{:S(2)}, u32[]{:S(2)}) collective-permute-start(f32[560,128]{1,0:T(8,128)S(1)} %copy-done.13), channel_id=1, source_target_pairs={{0,16},{1,17},{2,18},{3,19},{4,20},{5,21},{6,22},{7,23},{8,24},{9,... | collective-permute-start | bytes 860168 | tf_op jit(solution)/shard_map/ppermute | solution.py:413
  122.9 109.4 %collective-permute-start.14 = (f32[560,128]{1,0:T(8,128)}, f32[560,128]{1,0:T(8,128)S(1)}, u32[]{:S(2)}, u32[]{:S(2)}) collective-permute-start(f32[560,128]{1,0:T(8,128)} %get-tuple-element.56), channel_id=1, source_target_pairs={{0,17},{1,18},{2,19},{3,20},{4,21},{5,22},{6,23},{7,24},{8,25},{9,... | collective-permute-start | bytes 860168 | tf_op jit(solution)/shard_map/ppermute | solution.py:413
  123.6 108.7 %collective-permute-start.16 = (f32[560,128]{1,0:T(8,128)}, f32[560,128]{1,0:T(8,128)S(1)}, u32[]{:S(2)}, u32[]{:S(2)}) collective-permute-start(f32[560,128]{1,0:T(8,128)} %get-tuple-element.58), channel_id=1, source_target_pairs={{0,15},{1,16},{2,17},{3,18},{4,19},{5,20},{6,21},{7,22},{8,23},{9,... | collective-permute-start | bytes 860168 | tf_op jit(solution)/shard_map/ppermute | solution.py:413
  147.4 109.3 %collective-permute-start.12 = (f32[560,128]{1,0:T(8,128)}, f32[560,128]{1,0:T(8,128)S(1)}, u32[]{:S(2)}, u32[]{:S(2)}) collective-permute-start(f32[560,128]{1,0:T(8,128)} %get-tuple-element.54), channel_id=1, source_target_pairs={{0,19},{1,20},{2,21},{3,22},{4,23},{5,24},{6,25},{7,26},{8,27},{9,... | collective-permute-start | bytes 860168 | tf_op jit(solution)/shard_map/ppermute | solution.py:413
  149.1 125.7 %collective-permute-start.13 = (f32[560,128]{1,0:T(8,128)}, f32[560,128]{1,0:T(8,128)S(1)}, u32[]{:S(2)}, u32[]{:S(2)}) collective-permute-start(f32[560,128]{1,0:T(8,128)} %get-tuple-element.55), channel_id=1, source_target_pairs={{0,18},{1,19},{2,20},{3,21},{4,22},{5,23},{6,24},{7,25},{8,26},{9,... | collective-permute-start | bytes 860168 | tf_op jit(solution)/shard_map/ppermute | solution.py:413
  166.4 126.6 %collective-permute-start.17 = (f32[560,128]{1,0:T(8,128)}, f32[560,128]{1,0:T(8,128)S(1)}, u32[]{:S(2)}, u32[]{:S(2)}) collective-permute-start(f32[560,128]{1,0:T(8,128)} %get-tuple-element.59), channel_id=1, source_target_pairs={{0,14},{1,15},{2,16},{3,17},{4,18},{5,19},{6,20},{7,21},{8,22},{9,... | collective-permute-start | bytes 860168 | tf_op jit(solution)/shard_map/ppermute | solution.py:413
  232.3 62.7 %collective-permute-start.18 = (f32[560,128]{1,0:T(8,128)}, f32[560,128]{1,0:T(8,128)S(1)}, u32[]{:S(2)}, u32[]{:S(2)}) collective-permute-start(f32[560,128]{1,0:T(8,128)} %get-tuple-element.60), channel_id=1, source_target_pairs={{0,13},{1,14},{2,15},{3,16},{4,17},{5,18},{6,19},{7,20},{8,21},{9,... | collective-permute-start | bytes 860168 | tf_op jit(solution)/shard_map/ppermute | solution.py:413
  232.3 62.9 %collective-permute-start = (f32[560,128]{1,0:T(8,128)}, f32[560,128]{1,0:T(8,128)S(1)}, u32[]{:S(2)}, u32[]{:S(2)}) collective-permute-start(f32[560,128]{1,0:T(8,128)} %get-tuple-element.42), channel_id=1, source_target_pairs={{0,31},{1,0},{2,1},{3,2},{4,3},{5,4},{6,5},{7,6},{8,7},{9,8},{10,9... | collective-permute-start | bytes 860168 | tf_op jit(solution)/shard_map/ppermute | solution.py:413
  256.7 40.6 %collective-permute-start.1 = (f32[560,128]{1,0:T(8,128)}, f32[560,128]{1,0:T(8,128)S(1)}, u32[]{:S(2)}, u32[]{:S(2)}) collective-permute-start(f32[560,128]{1,0:T(8,128)} %get-tuple-element.43), channel_id=1, source_target_pairs={{0,30},{1,31},{2,0},{3,1},{4,2},{5,3},{6,4},{7,5},{8,6},{9,7},{10,... | collective-permute-start | bytes 860168 | tf_op jit(solution)/shard_map/ppermute | solution.py:413
  274.8 34.4 %collective-permute-start.2 = (f32[560,128]{1,0:T(8,128)}, f32[560,128]{1,0:T(8,128)S(1)}, u32[]{:S(2)}, u32[]{:S(2)}) collective-permute-start(f32[560,128]{1,0:T(8,128)} %get-tuple-element.44), channel_id=1, source_target_pairs={{0,29},{1,30},{2,31},{3,0},{4,1},{5,2},{6,3},{7,4},{8,5},{9,6},{10... | collective-permute-start | bytes 860168 | tf_op jit(solution)/shard_map/ppermute | solution.py:413
  293.0 30.7 %collective-permute-start.3 = (f32[560,128]{1,0:T(8,128)}, f32[560,128]{1,0:T(8,128)}, u32[]{:S(2)}, u32[]{:S(2)}) collective-permute-start(f32[560,128]{1,0:T(8,128)} %get-tuple-element.45), channel_id=1, source_target_pairs={{0,28},{1,29},{2,30},{3,31},{4,0},{5,1},{6,2},{7,3},{8,4},{9,5},{1... | collective-permute-start | bytes 860168 | tf_op jit(solution)/shard_map/ppermute | solution.py:413
  295.1 34.4 %collective-permute-start.4 = (f32[560,128]{1,0:T(8,128)}, f32[560,128]{1,0:T(8,128)}, u32[]{:S(2)}, u32[]{:S(2)}) collective-permute-start(f32[560,128]{1,0:T(8,128)} %get-tuple-element.46), channel_id=1, source_target_pairs={{0,27},{1,28},{2,29},{3,30},{4,31},{5,0},{6,1},{7,2},{8,3},{9,4},{... | collective-permute-start | bytes 860168 | tf_op jit(solution)/shard_map/ppermute | solution.py:413
  295.2 68.8 %collective-permute-start.5 = (f32[560,128]{1,0:T(8,128)}, f32[560,128]{1,0:T(8,128)}, u32[]{:S(2)}, u32[]{:S(2)}) collective-permute-start(f32[560,128]{1,0:T(8,128)} %get-tuple-element.47), channel_id=1, source_target_pairs={{0,26},{1,27},{2,28},{3,29},{4,30},{5,31},{6,0},{7,1},{8,2},{9,3},... | collective-permute-start | bytes 860168 | tf_op jit(solution)/shard_map/ppermute | solution.py:413
  297.3 73.4 %collective-permute-start.6 = (f32[560,128]{1,0:T(8,128)}, f32[560,128]{1,0:T(8,128)}, u32[]{:S(2)}, u32[]{:S(2)}) collective-permute-start(f32[560,128]{1,0:T(8,128)} %get-tuple-element.48), channel_id=1, source_target_pairs={{0,25},{1,26},{2,27},{3,28},{4,29},{5,30},{6,31},{7,0},{8,1},{9,2}... | collective-permute-start | bytes 860168 | tf_op jit(solution)/shard_map/ppermute | solution.py:413
  309.2 102.9 %collective-permute-start.7 = (f32[560,128]{1,0:T(8,128)}, f32[560,128]{1,0:T(8,128)}, u32[]{:S(2)}, u32[]{:S(2)}) collective-permute-start(f32[560,128]{1,0:T(8,128)} %get-tuple-element.49), channel_id=1, source_target_pairs={{0,24},{1,25},{2,26},{3,27},{4,28},{5,29},{6,30},{7,31},{8,0},{9,1... | collective-permute-start | bytes 860168 | tf_op jit(solution)/shard_map/ppermute | solution.py:413
  323.7 98.3 %collective-permute-start.8 = (f32[560,128]{1,0:T(8,128)}, f32[560,128]{1,0:T(8,128)}, u32[]{:S(2)}, u32[]{:S(2)}) collective-permute-start(f32[560,128]{1,0:T(8,128)} %get-tuple-element.50), channel_id=1, source_target_pairs={{0,23},{1,24},{2,25},{3,26},{4,27},{5,28},{6,29},{7,30},{8,31},{9,... | collective-permute-start | bytes 860168 | tf_op jit(solution)/shard_map/ppermute | solution.py:413
  329.4 134.8 %collective-permute-start.9 = (f32[560,128]{1,0:T(8,128)}, f32[560,128]{1,0:T(8,128)}, u32[]{:S(2)}, u32[]{:S(2)}) collective-permute-start(f32[560,128]{1,0:T(8,128)} %get-tuple-element.51), channel_id=1, source_target_pairs={{0,22},{1,23},{2,24},{3,25},{4,26},{5,27},{6,28},{7,29},{8,30},{9,... | collective-permute-start | bytes 860168 | tf_op jit(solution)/shard_map/ppermute | solution.py:413
  364.0 111.7 %collective-permute-start.10 = (f32[560,128]{1,0:T(8,128)}, f32[560,128]{1,0:T(8,128)}, u32[]{:S(2)}, u32[]{:S(2)}) collective-permute-start(f32[560,128]{1,0:T(8,128)} %get-tuple-element.52), channel_id=1, source_target_pairs={{0,21},{1,22},{2,23},{3,24},{4,25},{5,26},{6,27},{7,28},{8,29},{9,... | collective-permute-start | bytes 860168 | tf_op jit(solution)/shard_map/ppermute | solution.py:413
  370.7 161.5 %collective-permute-start.11 = (f32[560,128]{1,0:T(8,128)}, f32[560,128]{1,0:T(8,128)}, u32[]{:S(2)}, u32[]{:S(2)}) collective-permute-start(f32[560,128]{1,0:T(8,128)} %get-tuple-element.53), channel_id=1, source_target_pairs={{0,20},{1,21},{2,22},{3,23},{4,24},{5,25},{6,26},{7,27},{8,28},{9,... | collective-permute-start | bytes 860168 | tf_op jit(solution)/shard_map/ppermute | solution.py:413
  412.0 123.5 %collective-permute-start.19 = (f32[560,128]{1,0:T(8,128)}, f32[560,128]{1,0:T(8,128)}, u32[]{:S(2)}, u32[]{:S(2)}) collective-permute-start(f32[560,128]{1,0:T(8,128)} %get-tuple-element.61), channel_id=1, source_target_pairs={{0,12},{1,13},{2,14},{3,15},{4,16},{5,17},{6,18},{7,19},{8,20},{9,... | collective-permute-start | bytes 860168 | tf_op jit(solution)/shard_map/ppermute | solution.py:413
  422.0 113.6 %collective-permute-start.20 = (f32[560,128]{1,0:T(8,128)}, f32[560,128]{1,0:T(8,128)}, u32[]{:S(2)}, u32[]{:S(2)}) collective-permute-start(f32[560,128]{1,0:T(8,128)} %get-tuple-element.62), channel_id=1, source_target_pairs={{0,11},{1,12},{2,13},{3,14},{4,15},{5,16},{6,17},{7,18},{8,19},{9,... | collective-permute-start | bytes 860168 | tf_op jit(solution)/shard_map/ppermute | solution.py:413
  464.2 72.3 %collective-permute-start.21 = (f32[560,128]{1,0:T(8,128)}, f32[560,128]{1,0:T(8,128)}, u32[]{:S(2)}, u32[]{:S(2)}) collective-permute-start(f32[560,128]{1,0:T(8,128)} %get-tuple-element.63), channel_id=1, source_target_pairs={{0,10},{1,11},{2,12},{3,13},{4,14},{5,15},{6,16},{7,17},{8,18},{9,... | collective-permute-start | bytes 860168 | tf_op jit(solution)/shard_map/ppermute | solution.py:413
  475.7 66.1 %collective-permute-start.22 = (f32[560,128]{1,0:T(8,128)}, f32[560,128]{1,0:T(8,128)}, u32[]{:S(2)}, u32[]{:S(2)}) collective-permute-start(f32[560,128]{1,0:T(8,128)} %get-tuple-element.64), channel_id=1, source_target_pairs={{0,9},{1,10},{2,11},{3,12},{4,13},{5,14},{6,15},{7,16},{8,17},{9,1... | collective-permute-start | bytes 860168 | tf_op jit(solution)/shard_map/ppermute | solution.py:413
  532.3 27.3 %collective-permute-start.23 = (f32[560,128]{1,0:T(8,128)}, f32[560,128]{1,0:T(8,128)}, u32[]{:S(2)}, u32[]{:S(2)}) collective-permute-start(f32[560,128]{1,0:T(8,128)} %get-tuple-element.65), channel_id=1, source_target_pairs={{0,8},{1,9},{2,10},{3,11},{4,12},{5,13},{6,14},{7,15},{8,16},{9,17... | collective-permute-start | bytes 860168 | tf_op jit(solution)/shard_map/ppermute | solution.py:413
  535.5 60.8 %collective-permute-start.24 = (f32[560,128]{1,0:T(8,128)}, f32[560,128]{1,0:T(8,128)}, u32[]{:S(2)}, u32[]{:S(2)}) collective-permute-start(f32[560,128]{1,0:T(8,128)} %get-tuple-element.66), channel_id=1, source_target_pairs={{0,7},{1,8},{2,9},{3,10},{4,11},{5,12},{6,13},{7,14},{8,15},{9,16}... | collective-permute-start | bytes 860168 | tf_op jit(solution)/shard_map/ppermute | solution.py:413
  535.5 71.7 %collective-permute-start.25 = (f32[560,128]{1,0:T(8,128)}, f32[560,128]{1,0:T(8,128)}, u32[]{:S(2)}, u32[]{:S(2)}) collective-permute-start(f32[560,128]{1,0:T(8,128)} %get-tuple-element.67), channel_id=1, source_target_pairs={{0,6},{1,7},{2,8},{3,9},{4,10},{5,11},{6,12},{7,13},{8,14},{9,15},... | collective-permute-start | bytes 860168 | tf_op jit(solution)/shard_map/ppermute | solution.py:413
  536.5 80.0 %collective-permute-start.26 = (f32[560,128]{1,0:T(8,128)}, f32[560,128]{1,0:T(8,128)}, u32[]{:S(2)}, u32[]{:S(2)}) collective-permute-start(f32[560,128]{1,0:T(8,128)} %get-tuple-element.68), channel_id=1, source_target_pairs={{0,5},{1,6},{2,7},{3,8},{4,9},{5,10},{6,11},{7,12},{8,13},{9,14},{... | collective-permute-start | bytes 860168 | tf_op jit(solution)/shard_map/ppermute | solution.py:413
  541.7 88.4 %collective-permute-start.27 = (f32[560,128]{1,0:T(8,128)}, f32[560,128]{1,0:T(8,128)}, u32[]{:S(2)}, u32[]{:S(2)}) collective-permute-start(f32[560,128]{1,0:T(8,128)} %get-tuple-element.69), channel_id=1, source_target_pairs={{0,4},{1,5},{2,6},{3,7},{4,8},{5,9},{6,10},{7,11},{8,12},{9,13},{1... | collective-permute-start | bytes 860168 | tf_op jit(solution)/shard_map/ppermute | solution.py:413
  559.5 76.2 %collective-permute-start.28 = (f32[560,128]{1,0:T(8,128)}, f32[560,128]{1,0:T(8,128)}, u32[]{:S(2)}, u32[]{:S(2)}) collective-permute-start(f32[560,128]{1,0:T(8,128)} %get-tuple-element.70), channel_id=1, source_target_pairs={{0,3},{1,4},{2,5},{3,6},{4,7},{5,8},{6,9},{7,10},{8,11},{9,12},{10... | collective-permute-start | bytes 860168 | tf_op jit(solution)/shard_map/ppermute | solution.py:413
  596.4 46.4 %collective-permute-start.29 = (f32[560,128]{1,0:T(8,128)}, f32[560,128]{1,0:T(8,128)}, u32[]{:S(2)}, u32[]{:S(2)}) collective-permute-start(f32[560,128]{1,0:T(8,128)} %get-tuple-element.71), channel_id=1, source_target_pairs={{0,2},{1,3},{2,4},{3,5},{4,6},{5,7},{6,8},{7,9},{8,10},{9,11},{10,... | collective-permute-start | bytes 860168 | tf_op jit(solution)/shard_map/ppermute | solution.py:413
  607.3 37.3 %collective-permute-start.30 = (f32[560,128]{1,0:T(8,128)}, f32[560,128]{1,0:T(8,128)}, u32[]{:S(2)}, u32[]{:S(2)}) collective-permute-start(f32[560,128]{1,0:T(8,128)} %get-tuple-element.72), channel_id=1, source_target_pairs={{0,1},{1,2},{2,3},{3,4},{4,5},{5,6},{6,7},{7,8},{8,9},{9,10},{10,1... | collective-permute-start | bytes 860168 | tf_op jit(solution)/shard_map/ppermute | solution.py:413
  (14 other events, 4785.3 us)
where the time goes:
time: 663 us; the launch traced here: 659 us
  waiting for transfers between devices  372 us (56%)
  starting transfers between devices  146 us (22%)
  Pallas kernels  106 us (16%)
  blocking collectives  27.8 us (4%)
    ppermute x31, waiting for transfers between devices, shards(): lax.ppermute(block, 'wide', [(i, (i + s) % peers) for i in range(peers)])  372 us
    ppermute x31, starting transfers between devices, shards(): lax.ppermute(block, 'wide', [(i, (i + s) % peers) for i in range(peers)])  141 us
    pallas_call x1, Pallas kernels, rest_blocks(): pl.pallas_call(functools.partial(rest_kernel, shifts, peers, skipped), gr...  58.7 us
    pallas_call x3, Pallas kernels, early_blocks(): pl.pallas_call(functools.partial(early_kernel, shifts, peers, first), in_...  34.6 us
    all_to_all x1, blocking collectives, shards(): lax.all_to_all(sent, 'wide', 0, 0, tiled=True).reshape(peers * pairs)  27.8 us
  transfers between devices with their start and end apart: 32, of which 23 were waited for; matrix products, arithmetic and copies ran while one was open for 1% of the time, Pallas kernels for 5%

commit v1 on v0

--- a/solution.py
+++ b/solution.py
@@ -11,13 +11,14 @@
 TILE_S = 8
 LANES = 128
 CHUNKS = 5
-AHEAD = 2
+AHEAD = 3
 STEP = 40
 PACK = 280
 UNPACK = 80
 LAST = 40
 UNROLL = 2
-EARLY = (1, 2, 4)
+UNPACK_VMEM = 66_600_000
+EARLY = (2, 2, 3)
 
 
 SMEM = pl.BlockSpec(memory_space=pltpu.SMEM)
@@ -343,6 +344,7 @@
         + [pl.BlockSpec((UNPACK, LANES), lambda i: (i, 0))] * peers,
         out_specs=pl.BlockSpec((per, UNPACK, total), lambda i: (0, i, 0)),
         out_shape=jax.ShapeDtypeStruct((per, virtuals, total), jnp.float32),
+        compiler_params=pltpu.CompilerParams(vmem_limit_bytes=UNPACK_VMEM),
         name="unpack",
     )(pos, weights, *blocks)
 
@@ -382,9 +384,12 @@
 
 
 def order_of_shifts(peers):
-    shifts = [peers // 2]
-    for d in range(peers // 2 - 1, 0, -1):
+    middle = peers // 4
+    distances = [middle] + [d for d in range(peers // 2 - 1, 0, -1) if d != middle]
+    shifts = []
+    for d in distances:
         shifts += [d, peers - d]
+    shifts.insert(sum(EARLY), peers // 2)
     return shifts + [0]
 
 

time: 663 us -> 664 us (level)
  waiting for transfers between devices: 372 us -> 387 us
  starting transfers between devices: 146 us -> 138 us
    ppermute x31, waiting for transfers between devices: 372 us -> 387 us  [shards(): lax.ppermute(block, 'wide', [(i, (i + s) % peers) for i in range(peers)])]
    ppermute x31, starting transfers between devices: 141 us -> 132 us  [shards(): lax.ppermute(block, 'wide', [(i, (i + s) % peers) for i in range(peers)])]
  transfers between devices with their start and end apart: 32 -> 32, of which waited for: 23 -> 21; matrix products, arithmetic and copies ran while one was open for 1% -> 0% of each run, Pallas kernels for 5% -> 5%
where the time goes in v1:
time: 664 us; the launch traced here: 662 us
  waiting for transfers between devices  387 us (58%)
  starting transfers between devices  138 us (21%)
  Pallas kernels  105 us (16%)
  blocking collectives  27.8 us (4%)
    ppermute x31, waiting for transfers between devices, shards(): lax.ppermute(block, 'wide', [(i, (i + s) % peers) for i in range(peers)])  387 us
    ppermute x31, starting transfers between devices, shards(): lax.ppermute(block, 'wide', [(i, (i + s) % peers) for i in range(peers)])  132 us
    pallas_call x1, Pallas kernels, rest_blocks(): pl.pallas_call(functools.partial(rest_kernel, shifts, peers, skipped), gr...  58.8 us
    pallas_call x3, Pallas kernels, early_blocks(): pl.pallas_call(functools.partial(early_kernel, shifts, peers, first), in_...  33.3 us
    all_to_all x1, blocking collectives, shards(): lax.all_to_all(sent, 'wide', 0, 0, tiled=True).reshape(peers * pairs)  27.8 us
  transfers between devices with their start and end apart: 32, of which 21 were waited for; matrix products, arithmetic and copies ran while one was open for 0% of the time, Pallas kernels for 5%

profile of v1, /device:TPU:196, one launch (start us, length us, event | category | flops | bytes accessed | tf_op | source)
XLA Modules:
  0.0 661.7 jit_solution(15929617063992894188)
XLA Ops:
  0.6 10.9 %shard_map.68 = (f32[560,128]{1,0:T(8,128)}, f32[560,128]{1,0:T(8,128)}, bf16[600,800]{1,0:T(8,128)(2,1)}, bf16[600,800]{1,0:T(8,128)(2,1)}) custom-call(s32[1]{0:T(128)} %bitcast.3.pos, s32[64]{0:T(128)} %order.7, f32[8,800,512]{2,1,0:T(8,128)} %bitcast.6, f32[800,600]{1,0:T(8,128)} %refs_0_.1), custom_call_target="tpu_custom_call" | custom-call | flops 737280000 | bytes 13107200 | tf_op jit(solution)/shard_map/pallas_call | solution.py:146
  11.5 58.8 %rest_blocks.1 = (f32[560,128]{1,0:T(8,128)}, f32[560,128]{1,0:T(8,128)}, f32[560,128]{1,0:T(8,128)}, f32[560,128]{1,0:T(8,128)}, f32[560,128]{1,0:T(8,128)}, /*...) custom-call(s32[1]{0:T(128)} %bitcast.3.pos, ...), custom_call_target="tpu_custom_call" | custom-call | flops 11796480000 | bytes 13107200 | tf_op jit(solution)/shard_map/rest_blocks/pallas_call | solution.py:263
  71.2 27.8 %all_to_all.10 = f32[32,1,8]{2,1,0:T(1,128)S(1)} all-to-all(f32[32,1,8]{2,1,0:T(1,128)S(1)} %broadcast_in_dim.30), channel_id=1, replica_groups=mesh['groups'=4,'wide'=32] {'wide'}, dimensions={0} | all-to-all | bytes 2048 | tf_op jit(solution)/shard_map/all_to_all | solution.py:422
  111.0 9.7 %shard_map.70 = (f32[560,128]{1,0:T(8,128)}, f32[560,128]{1,0:T(8,128)}) custom-call(s32[1]{0:T(128)} %bitcast.3.pos, s32[64]{0:T(128)} %order.7, f32[8,800,512]{2,1,0:T(8,128)} %bitcast.8, bf16[600,800]{1,0:T(8,128)(2,1)} %get-tuple-element.38.v_high.refs_0_, bf16[600,800]{1,0:T(8,128)(2,1)} %get-tuple-element.39.v_low.refs_1_), custom_call_target="tpu_custom_call" | custom-call | flops 737280000 | bytes 13107200 | tf_op jit(solution)/shard_map/pallas_call | solution.py:146
  120.8 8.9 %collective-permute-start.14 = (f32[560,128]{1,0:T(8,128)}, f32[560,128]{1,0:T(8,128)}, u32[]{:S(2)}, u32[]{:S(2)}) collective-permute-start(f32[560,128]{1,0:T(8,128)} %get-tuple-element.56), channel_id=1, source_target_pairs={{0,17},{1,18},{2,19},{3,20},{4,21},{5,22},{6,23},{7,24},{8,25},{9,... | collective-permute-start | bytes 860168 | tf_op jit(solution)/shard_map/ppermute | solution.py:418
  130.5 12.7 %shard_map.69 = (f32[560,128]{1,0:T(8,128)}, f32[560,128]{1,0:T(8,128)}, f32[560,128]{1,0:T(8,128)}) custom-call(s32[1]{0:T(128)} %bitcast.3.pos, s32[64]{0:T(128)} %order.7, f32[8,800,512]{2,1,0:T(8,128)} %bitcast.9, bf16[600,800]{1,0:T(8,128)(2,1)} %get-tuple-element.38.v_high.refs_0_, bf16[600,800]{1,0:T(8,128)(2,1)} %get-tuple-element.39.v_low.refs_1_), custom_call_target="tpu_custom_call" | custom-call | flops 1105920000 | bytes 13107200 | tf_op jit(solution)/shard_map/pallas_call | solution.py:146
  143.2 8.8 %collective-permute-start.13 = (f32[560,128]{1,0:T(8,128)}, f32[560,128]{1,0:T(8,128)}, u32[]{:S(2)}, u32[]{:S(2)}) collective-permute-start(f32[560,128]{1,0:T(8,128)} %get-tuple-element.55), channel_id=1, source_target_pairs={{0,18},{1,19},{2,20},{3,21},{4,22},{5,23},{6,24},{7,25},{8,26},{9,... | collective-permute-start | bytes 860168 | tf_op jit(solution)/shard_map/ppermute | solution.py:418
  152.0 14.7 %collective-permute-done.7.refs_8_ = f32[560,128]{1,0:T(8,128)S(1)} collective-permute-done((f32[560,128]{1,0:T(8,128)}, f32[560,128]{1,0:T(8,128)S(1)}, u32[]{:S(2)}, u32[]{:S(2)}) %collective-permute-start.7) | collective-permute-done | bytes 286752 | tf_op jit(solution)/shard_map/ppermute | solution.py:418
  166.7 13.2 %collective-permute-done.23.refs_24_ = f32[560,128]{1,0:T(8,128)} collective-permute-done((f32[560,128]{1,0:T(8,128)}, f32[560,128]{1,0:T(8,128)}, u32[]{:S(2)}, u32[]{:S(2)}) %collective-permute-start.23) | collective-permute-done | bytes 286752 | tf_op jit(solution)/shard_map/ppermute | solution.py:418
  179.9 52.4 %collective-permute-done.14.refs_15_ = f32[560,128]{1,0:T(8,128)} collective-permute-done((f32[560,128]{1,0:T(8,128)}, f32[560,128]{1,0:T(8,128)}, u32[]{:S(2)}, u32[]{:S(2)}) %collective-permute-start.14) | collective-permute-done | bytes 286752 | tf_op jit(solution)/shard_map/ppermute | solution.py:418
  237.7 17.9 %collective-permute-start.2 = (f32[560,128]{1,0:T(8,128)}, f32[560,128]{1,0:T(8,128)}, u32[]{:S(2)}, u32[]{:S(2)}) collective-permute-start(f32[560,128]{1,0:T(8,128)} %get-tuple-element.44), channel_id=1, source_target_pairs={{0,29},{1,30},{2,31},{3,0},{4,1},{5,2},{6,3},{7,4},{8,5},{9,6},{10... | collective-permute-start | bytes 860168 | tf_op jit(solution)/shard_map/ppermute | solution.py:418
  255.6 14.1 %collective-permute-done.17.refs_18_ = f32[560,128]{1,0:T(8,128)} collective-permute-done((f32[560,128]{1,0:T(8,128)}, f32[560,128]{1,0:T(8,128)}, u32[]{:S(2)}, u32[]{:S(2)}) %collective-permute-start.17) | collective-permute-done | bytes 286752 | tf_op jit(solution)/shard_map/ppermute | solution.py:418
  269.8 9.7 %collective-permute-start.3 = (f32[560,128]{1,0:T(8,128)}, f32[560,128]{1,0:T(8,128)}, u32[]{:S(2)}, u32[]{:S(2)}) collective-permute-start(f32[560,128]{1,0:T(8,128)} %get-tuple-element.45), channel_id=1, source_target_pairs={{0,28},{1,29},{2,30},{3,31},{4,0},{5,1},{6,2},{7,3},{8,4},{9,5},{1... | collective-permute-start | bytes 860168 | tf_op jit(solution)/shard_map/ppermute | solution.py:418
  279.5 7.4 %collective-permute-done.18.refs_19_ = f32[560,128]{1,0:T(8,128)} collective-permute-done((f32[560,128]{1,0:T(8,128)}, f32[560,128]{1,0:T(8,128)}, u32[]{:S(2)}, u32[]{:S(2)}) %collective-permute-start.18) | collective-permute-done | bytes 286752 | tf_op jit(solution)/shard_map/ppermute | solution.py:418
  286.9 10.9 %collective-permute-start.4 = (f32[560,128]{1,0:T(8,128)}, f32[560,128]{1,0:T(8,128)}, u32[]{:S(2)}, u32[]{:S(2)}) collective-permute-start(f32[560,128]{1,0:T(8,128)} %get-tuple-element.46), channel_id=1, source_target_pairs={{0,27},{1,28},{2,29},{3,30},{4,31},{5,0},{6,1},{7,2},{8,3},{9,4},{... | collective-permute-start | bytes 860168 | tf_op jit(solution)/shard_map/ppermute | solution.py:418
  298.3 11.2 %collective-permute-start.9 = (f32[560,128]{1,0:T(8,128)}, f32[560,128]{1,0:T(8,128)}, u32[]{:S(2)}, u32[]{:S(2)}) collective-permute-start(f32[560,128]{1,0:T(8,128)} %get-tuple-element.51), channel_id=1, source_target_pairs={{0,22},{1,23},{2,24},{3,25},{4,26},{5,27},{6,28},{7,29},{8,30},{9,... | collective-permute-start | bytes 860168 | tf_op jit(solution)/shard_map/ppermute | solution.py:418
  309.5 7.1 %collective-permute-done.4.refs_5_ = f32[560,128]{1,0:T(8,128)} collective-permute-done((f32[560,128]{1,0:T(8,128)}, f32[560,128]{1,0:T(8,128)}, u32[]{:S(2)}, u32[]{:S(2)}) %collective-permute-start.4) | collective-permute-done | bytes 286752 | tf_op jit(solution)/shard_map/ppermute | solution.py:418
  316.6 8.8 %collective-permute-start.10 = (f32[560,128]{1,0:T(8,128)}, f32[560,128]{1,0:T(8,128)}, u32[]{:S(2)}, u32[]{:S(2)}) collective-permute-start(f32[560,128]{1,0:T(8,128)} %get-tuple-element.52), channel_id=1, source_target_pairs={{0,21},{1,22},{2,23},{3,24},{4,25},{5,26},{6,27},{7,28},{8,29},{9,... | collective-permute-start | bytes 860168 | tf_op jit(solution)/shard_map/ppermute | solution.py:418
  325.4 15.9 %collective-permute-done.5.refs_6_ = f32[560,128]{1,0:T(8,128)} collective-permute-done((f32[560,128]{1,0:T(8,128)}, f32[560,128]{1,0:T(8,128)}, u32[]{:S(2)}, u32[]{:S(2)}) %collective-permute-start.5) | collective-permute-done | bytes 286752 | tf_op jit(solution)/shard_map/ppermute | solution.py:418
  345.6 11.7 %collective-permute-done.6.refs_7_ = f32[560,128]{1,0:T(8,128)} collective-permute-done((f32[560,128]{1,0:T(8,128)}, f32[560,128]{1,0:T(8,128)}, u32[]{:S(2)}, u32[]{:S(2)}) %collective-permute-start.6) | collective-permute-done | bytes 286752 | tf_op jit(solution)/shard_map/ppermute | solution.py:418
  359.6 23.9 %collective-permute-done.8.refs_9_ = f32[560,128]{1,0:T(8,128)} collective-permute-done((f32[560,128]{1,0:T(8,128)}, f32[560,128]{1,0:T(8,128)}, u32[]{:S(2)}, u32[]{:S(2)}) %collective-permute-start.8) | collective-permute-done | bytes 286752 | tf_op jit(solution)/shard_map/ppermute | solution.py:418
  389.2 19.8 %collective-permute-done.9.refs_10_ = f32[560,128]{1,0:T(8,128)} collective-permute-done((f32[560,128]{1,0:T(8,128)}, f32[560,128]{1,0:T(8,128)}, u32[]{:S(2)}, u32[]{:S(2)}) %collective-permute-start.9) | collective-permute-done | bytes 286752 | tf_op jit(solution)/shard_map/ppermute | solution.py:418
  409.0 44.9 %collective-permute-done.10.refs_11_ = f32[560,128]{1,0:T(8,128)} collective-permute-done((f32[560,128]{1,0:T(8,128)}, f32[560,128]{1,0:T(8,128)}, u32[]{:S(2)}, u32[]{:S(2)}) %collective-permute-start.10) | collective-permute-done | bytes 286752 | tf_op jit(solution)/shard_map/ppermute | solution.py:418
  454.4 48.1 %collective-permute-done.11.refs_12_ = f32[560,128]{1,0:T(8,128)} collective-permute-done((f32[560,128]{1,0:T(8,128)}, f32[560,128]{1,0:T(8,128)}, u32[]{:S(2)}, u32[]{:S(2)}) %collective-permute-start.11) | collective-permute-done | bytes 286752 | tf_op jit(solution)/shard_map/ppermute | solution.py:418
  502.5 28.7 %collective-permute-done.12.refs_13_ = f32[560,128]{1,0:T(8,128)} collective-permute-done((f32[560,128]{1,0:T(8,128)}, f32[560,128]{1,0:T(8,128)}, u32[]{:S(2)}, u32[]{:S(2)}) %collective-permute-start.12) | collective-permute-done | bytes 286752 | tf_op jit(solution)/shard_map/ppermute | solution.py:418
  535.9 17.7 %collective-permute-start.25 = (f32[560,128]{1,0:T(8,128)S(1)}, f32[560,128]{1,0:T(8,128)}, u32[]{:S(2)}, u32[]{:S(2)}) collective-permute-start(f32[560,128]{1,0:T(8,128)S(1)} %copy-done.8), channel_id=1, source_target_pairs={{0,6},{1,7},{2,8},{3,9},{4,10},{5,11},{6,12},{7,13},{8,14},{9,15},... | collective-permute-start | bytes 860168 | tf_op jit(solution)/shard_map/ppermute | solution.py:418
  554.2 17.0 %collective-permute-start.28 = (f32[560,128]{1,0:T(8,128)S(1)}, f32[560,128]{1,0:T(8,128)}, u32[]{:S(2)}, u32[]{:S(2)}) collective-permute-start(f32[560,128]{1,0:T(8,128)S(1)} %copy-done.5), channel_id=1, source_target_pairs={{0,3},{1,4},{2,5},{3,6},{4,7},{5,8},{6,9},{7,10},{8,11},{9,12},{10... | collective-permute-start | bytes 860168 | tf_op jit(solution)/shard_map/ppermute | solution.py:418
  571.2 27.3 %collective-permute-done.24.refs_25_ = f32[560,128]{1,0:T(8,128)} collective-permute-done((f32[560,128]{1,0:T(8,128)S(1)}, f32[560,128]{1,0:T(8,128)}, u32[]{:S(2)}, u32[]{:S(2)}) %collective-permute-start.24) | collective-permute-done | bytes 286752 | tf_op jit(solution)/shard_map/ppermute | solution.py:418
  600.6 10.6 %collective-permute-done.26.refs_27_ = f32[560,128]{1,0:T(8,128)} collective-permute-done((f32[560,128]{1,0:T(8,128)S(1)}, f32[560,128]{1,0:T(8,128)}, u32[]{:S(2)}, u32[]{:S(2)}) %collective-permute-start.26) | collective-permute-done | bytes 286752 | tf_op jit(solution)/shard_map/ppermute | solution.py:418
  611.1 21.0 %collective-permute-done.27.refs_28_ = f32[560,128]{1,0:T(8,128)} collective-permute-done((f32[560,128]{1,0:T(8,128)S(1)}, f32[560,128]{1,0:T(8,128)}, u32[]{:S(2)}, u32[]{:S(2)}) %collective-permute-start.27) | collective-permute-done | bytes 286752 | tf_op jit(solution)/shard_map/ppermute | solution.py:418
  639.2 9.4 %collective-permute-done.29.refs_30_ = f32[560,128]{1,0:T(8,128)} collective-permute-done((f32[560,128]{1,0:T(8,128)S(1)}, f32[560,128]{1,0:T(8,128)}, u32[]{:S(2)}, u32[]{:S(2)}) %collective-permute-start.29) | collective-permute-done | bytes 286752 | tf_op jit(solution)/shard_map/ppermute | solution.py:418
  648.7 10.9 %unpack.1._ = f32[16,600,256]{2,1,0:T(8,128)} custom-call(s32[1]{0:T(128)} %bitcast.3.pos, f32[1,256]{1,0:T(1,128)} %bitcast.11, f32[560,128]{1,0:T(8,128)} %get-tuple-element.41.refs_0_, f32[560,128]{1,0:T(8,128)} %collective-permute-done.refs_1_, f32[560,128]{1,0:T(8,128)} %collective-permute-done.1.refs_2_, f32[560,128]{1,0:T(8,128)} %collective-permute-done.2.refs_3_, ...), custom_call_target="tpu_custom_call" | custom-call | tf_op jit(solution)/shard_map/unpack/pallas_call | solution.py:340
  (73 shorter events, 49.0 us)
Async XLA Ops:
  99.1 560.5 %all-to-all-start = ((f32[32,40,128]{2,1,0:T(8,128)}), f32[32,40,128]{2,1,0:T(8,128)}, u32[]{:S(2)}, u32[]{:S(2)}) async-start(f32[32,40,128]{2,1,0:T(8,128)} %get-tuple-element.40), calls=%async_computation | async-start | bytes 1310720 | tf_op jit(solution)/shard_map/all_to_all | solution.py:423
  104.9 61.8 %collective-permute-start.7 = (f32[560,128]{1,0:T(8,128)}, f32[560,128]{1,0:T(8,128)S(1)}, u32[]{:S(2)}, u32[]{:S(2)}) collective-permute-start(f32[560,128]{1,0:T(8,128)} %get-tuple-element.49), channel_id=1, source_target_pairs={{0,24},{1,25},{2,26},{3,27},{4,28},{5,29},{6,30},{7,31},{8,0},{9,1... | collective-permute-start | bytes 860168 | tf_op jit(solution)/shard_map/ppermute | solution.py:418
  110.0 69.9 %collective-permute-start.23 = (f32[560,128]{1,0:T(8,128)}, f32[560,128]{1,0:T(8,128)}, u32[]{:S(2)}, u32[]{:S(2)}) collective-permute-start(f32[560,128]{1,0:T(8,128)} %get-tuple-element.65), channel_id=1, source_target_pairs={{0,8},{1,9},{2,10},{3,11},{4,12},{5,13},{6,14},{7,15},{8,16},{9,17... | collective-permute-start | bytes 860168 | tf_op jit(solution)/shard_map/ppermute | solution.py:418
  120.8 111.5 %collective-permute-start.14 = (f32[560,128]{1,0:T(8,128)}, f32[560,128]{1,0:T(8,128)}, u32[]{:S(2)}, u32[]{:S(2)}) collective-permute-start(f32[560,128]{1,0:T(8,128)} %get-tuple-element.56), channel_id=1, source_target_pairs={{0,17},{1,18},{2,19},{3,20},{4,21},{5,22},{6,23},{7,24},{8,25},{9,... | collective-permute-start | bytes 860168 | tf_op jit(solution)/shard_map/ppermute | solution.py:418
  129.7 102.6 %collective-permute-start.16 = (f32[560,128]{1,0:T(8,128)}, f32[560,128]{1,0:T(8,128)}, u32[]{:S(2)}, u32[]{:S(2)}) collective-permute-start(f32[560,128]{1,0:T(8,128)} %get-tuple-element.58), channel_id=1, source_target_pairs={{0,15},{1,16},{2,17},{3,18},{4,19},{5,20},{6,21},{7,22},{8,23},{9,... | collective-permute-start | bytes 860168 | tf_op jit(solution)/shard_map/ppermute | solution.py:418
  143.2 94.5 %collective-permute-start.13 = (f32[560,128]{1,0:T(8,128)}, f32[560,128]{1,0:T(8,128)}, u32[]{:S(2)}, u32[]{:S(2)}) collective-permute-start(f32[560,128]{1,0:T(8,128)} %get-tuple-element.55), channel_id=1, source_target_pairs={{0,18},{1,19},{2,20},{3,21},{4,22},{5,23},{6,24},{7,25},{8,26},{9,... | collective-permute-start | bytes 860168 | tf_op jit(solution)/shard_map/ppermute | solution.py:418
  166.7 103.1 %collective-permute-start.17 = (f32[560,128]{1,0:T(8,128)}, f32[560,128]{1,0:T(8,128)}, u32[]{:S(2)}, u32[]{:S(2)}) collective-permute-start(f32[560,128]{1,0:T(8,128)} %get-tuple-element.59), channel_id=1, source_target_pairs={{0,14},{1,15},{2,16},{3,17},{4,18},{5,19},{6,20},{7,21},{8,22},{9,... | collective-permute-start | bytes 860168 | tf_op jit(solution)/shard_map/ppermute | solution.py:418
  179.9 107.0 %collective-permute-start.18 = (f32[560,128]{1,0:T(8,128)}, f32[560,128]{1,0:T(8,128)}, u32[]{:S(2)}, u32[]{:S(2)}) collective-permute-start(f32[560,128]{1,0:T(8,128)} %get-tuple-element.60), channel_id=1, source_target_pairs={{0,13},{1,14},{2,15},{3,16},{4,17},{5,18},{6,19},{7,20},{8,21},{9,... | collective-permute-start | bytes 860168 | tf_op jit(solution)/shard_map/ppermute | solution.py:418
  232.3 65.6 %collective-permute-start = (f32[560,128]{1,0:T(8,128)}, f32[560,128]{1,0:T(8,128)}, u32[]{:S(2)}, u32[]{:S(2)}) collective-permute-start(f32[560,128]{1,0:T(8,128)} %get-tuple-element.42), channel_id=1, source_target_pairs={{0,31},{1,0},{2,1},{3,2},{4,3},{5,4},{6,5},{7,6},{8,7},{9,8},{10,9... | collective-permute-start | bytes 860168 | tf_op jit(solution)/shard_map/ppermute | solution.py:418
  232.3 65.8 %collective-permute-start.1 = (f32[560,128]{1,0:T(8,128)}, f32[560,128]{1,0:T(8,128)}, u32[]{:S(2)}, u32[]{:S(2)}) collective-permute-start(f32[560,128]{1,0:T(8,128)} %get-tuple-element.43), channel_id=1, source_target_pairs={{0,30},{1,31},{2,0},{3,1},{4,2},{5,3},{6,4},{7,5},{8,6},{9,7},{10,... | collective-permute-start | bytes 860168 | tf_op jit(solution)/shard_map/ppermute | solution.py:418
  237.7 60.3 %collective-permute-start.2 = (f32[560,128]{1,0:T(8,128)}, f32[560,128]{1,0:T(8,128)}, u32[]{:S(2)}, u32[]{:S(2)}) collective-permute-start(f32[560,128]{1,0:T(8,128)} %get-tuple-element.44), channel_id=1, source_target_pairs={{0,29},{1,30},{2,31},{3,0},{4,1},{5,2},{6,3},{7,4},{8,5},{9,6},{10... | collective-permute-start | bytes 860168 | tf_op jit(solution)/shard_map/ppermute | solution.py:418
  269.8 28.5 %collective-permute-start.3 = (f32[560,128]{1,0:T(8,128)}, f32[560,128]{1,0:T(8,128)}, u32[]{:S(2)}, u32[]{:S(2)}) collective-permute-start(f32[560,128]{1,0:T(8,128)} %get-tuple-element.45), channel_id=1, source_target_pairs={{0,28},{1,29},{2,30},{3,31},{4,0},{5,1},{6,2},{7,3},{8,4},{9,5},{1... | collective-permute-start | bytes 860168 | tf_op jit(solution)/shard_map/ppermute | solution.py:418
  286.9 29.6 %collective-permute-start.4 = (f32[560,128]{1,0:T(8,128)}, f32[560,128]{1,0:T(8,128)}, u32[]{:S(2)}, u32[]{:S(2)}) collective-permute-start(f32[560,128]{1,0:T(8,128)} %get-tuple-element.46), channel_id=1, source_target_pairs={{0,27},{1,28},{2,29},{3,30},{4,31},{5,0},{6,1},{7,2},{8,3},{9,4},{... | collective-permute-start | bytes 860168 | tf_op jit(solution)/shard_map/ppermute | solution.py:418
  297.9 43.4 %collective-permute-start.5 = (f32[560,128]{1,0:T(8,128)}, f32[560,128]{1,0:T(8,128)}, u32[]{:S(2)}, u32[]{:S(2)}) collective-permute-start(f32[560,128]{1,0:T(8,128)} %get-tuple-element.47), channel_id=1, source_target_pairs={{0,26},{1,27},{2,28},{3,29},{4,30},{5,31},{6,0},{7,1},{8,2},{9,3},... | collective-permute-start | bytes 860168 | tf_op jit(solution)/shard_map/ppermute | solution.py:418
  298.0 59.2 %collective-permute-start.6 = (f32[560,128]{1,0:T(8,128)}, f32[560,128]{1,0:T(8,128)}, u32[]{:S(2)}, u32[]{:S(2)}) collective-permute-start(f32[560,128]{1,0:T(8,128)} %get-tuple-element.48), channel_id=1, source_target_pairs={{0,25},{1,26},{2,27},{3,28},{4,29},{5,30},{6,31},{7,0},{8,1},{9,2}... | collective-permute-start | bytes 860168 | tf_op jit(solution)/shard_map/ppermute | solution.py:418
  298.1 85.5 %collective-permute-start.8 = (f32[560,128]{1,0:T(8,128)}, f32[560,128]{1,0:T(8,128)}, u32[]{:S(2)}, u32[]{:S(2)}) collective-permute-start(f32[560,128]{1,0:T(8,128)} %get-tuple-element.50), channel_id=1, source_target_pairs={{0,23},{1,24},{2,25},{3,26},{4,27},{5,28},{6,29},{7,30},{8,31},{9,... | collective-permute-start | bytes 860168 | tf_op jit(solution)/shard_map/ppermute | solution.py:418
  298.3 110.7 %collective-permute-start.9 = (f32[560,128]{1,0:T(8,128)}, f32[560,128]{1,0:T(8,128)}, u32[]{:S(2)}, u32[]{:S(2)}) collective-permute-start(f32[560,128]{1,0:T(8,128)} %get-tuple-element.51), channel_id=1, source_target_pairs={{0,22},{1,23},{2,24},{3,25},{4,26},{5,27},{6,28},{7,29},{8,30},{9,... | collective-permute-start | bytes 860168 | tf_op jit(solution)/shard_map/ppermute | solution.py:418
  316.6 137.3 %collective-permute-start.10 = (f32[560,128]{1,0:T(8,128)}, f32[560,128]{1,0:T(8,128)}, u32[]{:S(2)}, u32[]{:S(2)}) collective-permute-start(f32[560,128]{1,0:T(8,128)} %get-tuple-element.52), channel_id=1, source_target_pairs={{0,21},{1,22},{2,23},{3,24},{4,25},{5,26},{6,27},{7,28},{8,29},{9,... | collective-permute-start | bytes 860168 | tf_op jit(solution)/shard_map/ppermute | solution.py:418
  341.3 161.2 %collective-permute-start.11 = (f32[560,128]{1,0:T(8,128)}, f32[560,128]{1,0:T(8,128)}, u32[]{:S(2)}, u32[]{:S(2)}) collective-permute-start(f32[560,128]{1,0:T(8,128)} %get-tuple-element.53), channel_id=1, source_target_pairs={{0,20},{1,21},{2,22},{3,23},{4,24},{5,25},{6,26},{7,27},{8,28},{9,... | collective-permute-start | bytes 860168 | tf_op jit(solution)/shard_map/ppermute | solution.py:418
  357.3 173.9 %collective-permute-start.12 = (f32[560,128]{1,0:T(8,128)}, f32[560,128]{1,0:T(8,128)}, u32[]{:S(2)}, u32[]{:S(2)}) collective-permute-start(f32[560,128]{1,0:T(8,128)} %get-tuple-element.54), channel_id=1, source_target_pairs={{0,19},{1,20},{2,21},{3,22},{4,23},{5,24},{6,25},{7,26},{8,27},{9,... | collective-permute-start | bytes 860168 | tf_op jit(solution)/shard_map/ppermute | solution.py:418
  383.5 152.3 %collective-permute-start.15 = (f32[560,128]{1,0:T(8,128)}, f32[560,128]{1,0:T(8,128)}, u32[]{:S(2)}, u32[]{:S(2)}) collective-permute-start(f32[560,128]{1,0:T(8,128)} %get-tuple-element.57), channel_id=1, source_target_pairs={{0,16},{1,17},{2,18},{3,19},{4,20},{5,21},{6,22},{7,23},{8,24},{9,... | collective-permute-start | bytes 860168 | tf_op jit(solution)/shard_map/ppermute | solution.py:418
  409.0 126.9 %collective-permute-start.19 = (f32[560,128]{1,0:T(8,128)}, f32[560,128]{1,0:T(8,128)}, u32[]{:S(2)}, u32[]{:S(2)}) collective-permute-start(f32[560,128]{1,0:T(8,128)} %get-tuple-element.61), channel_id=1, source_target_pairs={{0,12},{1,13},{2,14},{3,15},{4,16},{5,17},{6,18},{7,19},{8,20},{9,... | collective-permute-start | bytes 860168 | tf_op jit(solution)/shard_map/ppermute | solution.py:418
  453.9 99.7 %collective-permute-start.20 = (f32[560,128]{1,0:T(8,128)S(1)}, f32[560,128]{1,0:T(8,128)}, u32[]{:S(2)}, u32[]{:S(2)}) collective-permute-start(f32[560,128]{1,0:T(8,128)S(1)} %copy-done.12), channel_id=1, source_target_pairs={{0,11},{1,12},{2,13},{3,14},{4,15},{5,16},{6,17},{7,18},{8,19},{9,... | collective-permute-start | bytes 860168 | tf_op jit(solution)/shard_map/ppermute | solution.py:418
  502.5 51.4 %collective-permute-start.21 = (f32[560,128]{1,0:T(8,128)S(1)}, f32[560,128]{1,0:T(8,128)}, u32[]{:S(2)}, u32[]{:S(2)}) collective-permute-start(f32[560,128]{1,0:T(8,128)S(1)} %copy-done.11), channel_id=1, source_target_pairs={{0,10},{1,11},{2,12},{3,13},{4,14},{5,15},{6,16},{7,17},{8,18},{9,... | collective-permute-start | bytes 860168 | tf_op jit(solution)/shard_map/ppermute | solution.py:418
  531.2 23.0 %collective-permute-start.22 = (f32[560,128]{1,0:T(8,128)S(1)}, f32[560,128]{1,0:T(8,128)}, u32[]{:S(2)}, u32[]{:S(2)}) collective-permute-start(f32[560,128]{1,0:T(8,128)S(1)} %copy-done.10), channel_id=1, source_target_pairs={{0,9},{1,10},{2,11},{3,12},{4,13},{5,14},{6,15},{7,16},{8,17},{9,1... | collective-permute-start | bytes 860168 | tf_op jit(solution)/shard_map/ppermute | solution.py:418
  535.9 62.6 %collective-permute-start.24 = (f32[560,128]{1,0:T(8,128)S(1)}, f32[560,128]{1,0:T(8,128)}, u32[]{:S(2)}, u32[]{:S(2)}) collective-permute-start(f32[560,128]{1,0:T(8,128)S(1)} %copy-done.9), channel_id=1, source_target_pairs={{0,7},{1,8},{2,9},{3,10},{4,11},{5,12},{6,13},{7,14},{8,15},{9,16}... | collective-permute-start | bytes 860168 | tf_op jit(solution)/shard_map/ppermute | solution.py:418
  535.9 62.6 %collective-permute-start.25 = (f32[560,128]{1,0:T(8,128)S(1)}, f32[560,128]{1,0:T(8,128)}, u32[]{:S(2)}, u32[]{:S(2)}) collective-permute-start(f32[560,128]{1,0:T(8,128)S(1)} %copy-done.8), channel_id=1, source_target_pairs={{0,6},{1,7},{2,8},{3,9},{4,10},{5,11},{6,12},{7,13},{8,14},{9,15},... | collective-permute-start | bytes 860168 | tf_op jit(solution)/shard_map/ppermute | solution.py:418
  553.7 57.5 %collective-permute-start.26 = (f32[560,128]{1,0:T(8,128)S(1)}, f32[560,128]{1,0:T(8,128)}, u32[]{:S(2)}, u32[]{:S(2)}) collective-permute-start(f32[560,128]{1,0:T(8,128)S(1)} %copy-done.7), channel_id=1, source_target_pairs={{0,5},{1,6},{2,7},{3,8},{4,9},{5,10},{6,11},{7,12},{8,13},{9,14},{... | collective-permute-start | bytes 860168 | tf_op jit(solution)/shard_map/ppermute | solution.py:418
  553.9 78.3 %collective-permute-start.27 = (f32[560,128]{1,0:T(8,128)S(1)}, f32[560,128]{1,0:T(8,128)}, u32[]{:S(2)}, u32[]{:S(2)}) collective-permute-start(f32[560,128]{1,0:T(8,128)S(1)} %copy-done.6), channel_id=1, source_target_pairs={{0,4},{1,5},{2,6},{3,7},{4,8},{5,9},{6,10},{7,11},{8,12},{9,13},{1... | collective-permute-start | bytes 860168 | tf_op jit(solution)/shard_map/ppermute | solution.py:418
  554.2 85.0 %collective-permute-start.28 = (f32[560,128]{1,0:T(8,128)S(1)}, f32[560,128]{1,0:T(8,128)}, u32[]{:S(2)}, u32[]{:S(2)}) collective-permute-start(f32[560,128]{1,0:T(8,128)S(1)} %copy-done.5), channel_id=1, source_target_pairs={{0,3},{1,4},{2,5},{3,6},{4,7},{5,8},{6,9},{7,10},{8,11},{9,12},{10... | collective-permute-start | bytes 860168 | tf_op jit(solution)/shard_map/ppermute | solution.py:418
  598.4 50.2 %collective-permute-start.29 = (f32[560,128]{1,0:T(8,128)S(1)}, f32[560,128]{1,0:T(8,128)}, u32[]{:S(2)}, u32[]{:S(2)}) collective-permute-start(f32[560,128]{1,0:T(8,128)S(1)} %copy-done.4), channel_id=1, source_target_pairs={{0,2},{1,3},{2,4},{3,5},{4,6},{5,7},{6,8},{7,9},{8,10},{9,11},{10,... | collective-permute-start | bytes 860168 | tf_op jit(solution)/shard_map/ppermute | solution.py:418
  598.5 50.2 %collective-permute-start.30 = (f32[560,128]{1,0:T(8,128)S(1)}, f32[560,128]{1,0:T(8,128)}, u32[]{:S(2)}, u32[]{:S(2)}) collective-permute-start(f32[560,128]{1,0:T(8,128)S(1)} %copy-done.3), channel_id=1, source_target_pairs={{0,1},{1,2},{2,3},{3,4},{4,5},{5,6},{6,7},{7,8},{8,9},{9,10},{10,1... | collective-permute-start | bytes 860168 | tf_op jit(solution)/shard_map/ppermute | solution.py:418
  (13 other events, 5603.2 us)
